TPU v7x, 32 devices: a whole 2x2x4 slice. The times are simulated.
32 devices in a mesh: seq: 8 (over z, x), tensor: 4 (over y, core).
Axes of the slice: x: 2, y: 2, z: 4, core: 2. Of those that a mesh axis runs over, the one named last changes fastest.
Arguments:
- tokens: bfloat16 [4096, 2048], P('seq', 'tensor'), may hold values from -12 to 12
- attn_gain: float32 [2048], replicated, may hold values from 0.1 to 1.9
- w_query: bfloat16 [2048, 2048], P('seq', 'tensor'), as said below
- w_key: bfloat16 [2048, 512], P('seq', 'tensor'), as said below
- w_value: bfloat16 [2048, 512], P('seq', 'tensor'), may hold values from -0.125 to 0.125
- w_out: bfloat16 [2048, 2048], P('tensor', 'seq'), may hold values from -0.125 to 0.125
- mlp_gain: float32 [2048], replicated, may hold values from 0.1 to 1.9
- w_gate: bfloat16 [2048, 5632], P('seq', 'tensor'), may hold values from -0.125 to 0.125
- w_up: bfloat16 [2048, 5632], P('seq', 'tensor'), may hold values from -0.125 to 0.125
- w_down: bfloat16 [5632, 2048], P('tensor', 'seq'), may hold values from -0.078125 to 0.078125
Outputs:
- layer_out: bfloat16 [4096, 2048], P('seq', 'tensor')
Inputs may be any that keep to these rules, and one draw needn't show every extreme that they name: `w_query`: entries are of order 2048 to the power -1/2. `w_key`: entries are of order 2048 to the power -1/2.
All inputs are finite; a program needn't handle non-finite values.
Results may differ from a plain program's by a relative error of at most 0.013.
Values may be sent and summed in bfloat16 or wider, within the bound.
A program may use at most 128 MiB of HBM per device.

v0:
```python
import jax
import jax.numpy as jnp
from jax import lax
from jax.sharding import PartitionSpec as P

HEAD_DIM = 128
WINDOW = 1024


def passed_along(block, axis, distance):
    devices = range(lax.axis_size(axis))
    route = [(i - distance, i) for i in devices if i - distance in devices]
    return lax.ppermute(block, axis, route)


def scaled_rows(values, gain):
    values = values.astype(jnp.float32)
    mean_square = jnp.mean(values * values, axis=1, keepdims=True)
    return (values * lax.rsqrt(mean_square + 1e-06) * gain).astype(jnp.bfloat16)


def product(left, right):
    return jnp.dot(left, right, preferred_element_type=jnp.float32)


def window_attention(queries, context_keys, context_values, reach, position):
    rows = queries.shape[0]
    local_kv = context_keys.shape[1] // HEAD_DIM
    group = queries.shape[1] // (local_kv * HEAD_DIM)
    block = min(512, rows)
    span = WINDOW + block
    scale = HEAD_DIM ** (-0.5)
    start = reach * rows - WINDOW
    query_block = queries.reshape(block, local_kv, group, HEAD_DIM)
    key_block = context_keys.reshape(span, local_kv, HEAD_DIM)
    value_block = context_values.reshape(span, local_kv, HEAD_DIM)
    scores = (
        jnp.einsum("qkgd,ckd->kgqc", query_block, key_block, preferred_element_type=jnp.float32)
        * scale
    )
    query_pos = lax.broadcasted_iota(jnp.int32, (block, span), 0)
    key_pos = lax.broadcasted_iota(jnp.int32, (block, span), 1)
    distance = query_pos + WINDOW - key_pos
    first_key = (position - reach) * rows + start
    allowed = (distance >= 0) & (distance < WINDOW) & (key_pos + first_key >= 0)
    scores = jnp.where(allowed[None, None], scores, -1e30)
    highest = jnp.max(scores, axis=3, keepdims=True)
    raised = jnp.exp(scores - highest)
    weights = (raised / jnp.sum(raised, axis=3, keepdims=True)).astype(jnp.bfloat16)
    mixed = jnp.einsum("kgqc,ckd->qkgd", weights, value_block, preferred_element_type=jnp.float32)
    outputs = mixed.astype(jnp.bfloat16).reshape(block, local_kv * group * HEAD_DIM)
    return outputs


def per_device(tokens, attn_gain, w_query, w_key, w_value, w_out, mlp_gain, w_gate, w_up, w_down):
    rows = tokens.shape[0]
    whole = lax.all_gather(tokens, "tensor", axis=1, tiled=True)
    normed = scaled_rows(whole, attn_gain)
    query_full = lax.all_gather(w_query, "seq", axis=0, tiled=True)
    key_full, value_full = (
        lax.all_gather(w_key, "seq", axis=0, tiled=True),
        lax.all_gather(w_value, "seq", axis=0, tiled=True),
    )
    queries = product(normed, query_full).astype(jnp.bfloat16)
    keys = product(normed, key_full).astype(jnp.bfloat16)
    values = product(normed, value_full).astype(jnp.bfloat16)
    reach = -(-WINDOW // rows)
    earlier = []
    for step in range(reach):
        earlier.append(passed_along((keys, values), "seq", step + 1))
    context_keys = jnp.concatenate(
        [earlier[reach - 1 - step][0] for step in range(reach)] + [keys], axis=0
    )
    context_values = jnp.concatenate(
        [earlier[reach - 1 - step][1] for step in range(reach)] + [values], axis=0
    )
    position = lax.axis_index("seq")
    attended = window_attention(queries, context_keys, context_values, reach, position)
    out_full = lax.all_gather(w_out, "seq", axis=1, tiled=True)
    head_terms = product(attended, out_full)
    share = tokens.shape[1]
    attn_whole = lax.psum(head_terms.astype(jnp.bfloat16), "tensor").astype(jnp.float32)
    stream_whole = (whole.astype(jnp.float32) + attn_whole).astype(jnp.bfloat16)
    stream_share = lax.dynamic_slice_in_dim(
        stream_whole, lax.axis_index("tensor") * share, share, 1
    )
    stream_normed = scaled_rows(stream_whole, mlp_gain)
    gate_full = lax.all_gather(w_gate, "seq", axis=0, tiled=True)
    up_full = lax.all_gather(w_up, "seq", axis=0, tiled=True)
    gate = product(stream_normed, gate_full)
    upward = product(stream_normed, up_full)
    hidden = (jax.nn.silu(gate) * upward).astype(jnp.bfloat16)
    down_full = lax.all_gather(w_down, "seq", axis=1, tiled=True)
    unit_terms = product(hidden, down_full)
    mlp_share = lax.psum_scatter(
        unit_terms.astype(jnp.bfloat16), "tensor", scatter_dimension=1, tiled=True
    ).astype(jnp.float32)
    return (stream_share.astype(jnp.float32) + mlp_share).astype(jnp.bfloat16)


def solution(mesh):
    in_specs = (
        P("seq", "tensor"),
        P(),
        P("seq", "tensor"),
        P("seq", "tensor"),
        P("seq", "tensor"),
        P("tensor", "seq"),
        P(),
        P("seq", "tensor"),
        P("seq", "tensor"),
        P("tensor", "seq"),
    )
    out_specs = P("seq", "tensor")
    return jax.shard_map(
        per_device, mesh=mesh, in_specs=in_specs, out_specs=out_specs, check_vma=False
    )
```

profile of v0, /device:TPU:0, one launch (start us, length us, event | category | flops | bytes accessed | tf_op | source)
XLA Modules:
  0.0 529.0 jit_solution(15447656682437301794)
XLA Ops:
  8.8 33.4 %all_gather.26 = bf16[2048,128]{1,0:T(8,128)(2,1)S(1)} all-gather(bf16[256,128]{1,0:T(8,128)(2,1)} %param.13), channel_id=1, replica_groups=mesh['seq'=8,'tensor'=4] {'seq'}, dimensions={0}, use_global_device_ids=true | all-gather | bytes 589824 | tf_op jit(solution)/shard_map/all_gather | solution.py:61
  42.2 35.2 %all_gather.25 = bf16[2048,128]{1,0:T(8,128)(2,1)} all-gather(bf16[256,128]{1,0:T(8,128)(2,1)} %param.14), channel_id=1, replica_groups=mesh['seq'=8,'tensor'=4] {'seq'}, dimensions={0}, use_global_device_ids=true | all-gather | bytes 589824 | tf_op jit(solution)/shard_map/all_gather | solution.py:62
  77.3 1.3 fusion.14
  78.7 2.2 fusion.7
  80.9 2.4 convolution_convert_fusion.3
  83.3 1.3 collective-permute-start.2
  84.6 4.3 collective-permute-start.3
  89.6 2.7 collective-permute-start
  92.4 2.7 collective-permute-start.1
  95.1 3.0 convolution_convert_fusion.2
  98.1 3.3 fusion.1
  101.4 2.8 fusion
  104.2 4.8 fusion.16
  109.0 33.7 %all-gather.11.cloned.1.call-done = bf16[512,2048]{1,0:T(8,128)(2,1)} async-done(((bf16[512,256]{1,0:T(8,128)(2,1)}), bf16[512,2048]{1,0:T(8,128)(2,1)}) %all-gather.11.cloned.1.call-update) | async-done | bytes 2097168 | tf_op jit(solution)/shard_map/all_gather | solution.py:79
  142.7 4.4 convolution_convert_fusion
  149.3 47.5 %all-reduce.2.cloned.1.call-done = bf16[512,2048]{1,0:T(8,128)(2,1)} async-done(((bf16[512,2048]{1,0:T(8,128)(2,1)}), bf16[512,2048]{1,0:T(8,128)(2,1)}) %all-reduce.2.cloned.1.call-update) | async-done | bytes 2097168 | tf_op jit(solution)/shard_map/psum | solution.py:82
  196.9 3.9 fusion.4
  200.8 90.5 %all-gather.13.cloned.1.call-done = bf16[2048,1408]{1,0:T(8,128)(2,1)} async-done(((bf16[256,1408]{1,0:T(8,128)(2,1)}), bf16[2048,1408]{1,0:T(8,128)(2,1)}) %all-gather.13.cloned.1.call-update) | async-done | bytes 5767184 | tf_op jit(solution)/shard_map/all_gather | solution.py:88
  291.3 8.4 %fusion.21 = f32[512,1408]{1,0:T(8,128)} fusion(bf16[2048,1408]{1,0:T(8,128)(2,1)} %all-gather.13.cloned.1.call-done, bf16[512,2048]{1,0:T(8,128)(2,1)} %get-tuple-element.6, f32[2048]{0:T(1024)S(1)} %copy-done.4, f32[512]{0:T(512)S(1)} %add_rsqrt_fusion), kind=kOutput, calls=%fused_computation.33 | convolution fusion | flops 2956984320 | bytes 10758144 | tf_op jit(solution)/shard_map/dot_general | solution.py:23
  299.7 84.1 %all-gather.15.cloned.1.call-done = bf16[2048,1408]{1,0:T(8,128)(2,1)} async-done(((bf16[256,1408]{1,0:T(8,128)(2,1)}), bf16[2048,1408]{1,0:T(8,128)(2,1)}) %all-gather.15.cloned.1.call-update) | async-done | bytes 5767184 | tf_op jit(solution)/shard_map/all_gather | solution.py:89
  383.9 93.4 %all-gather.17.cloned.1.call-done = bf16[1408,2048]{1,0:T(8,128)(2,1)} async-done(((bf16[1408,256]{1,0:T(8,128)(2,1)}), bf16[1408,2048]{1,0:T(8,128)(2,1)}) %all-gather.17.cloned.1.call-update) | async-done | bytes 5767184 | tf_op jit(solution)/shard_map/all_gather | solution.py:93
  477.2 13.4 %convolution_convert_fusion.1 = bf16[512,2048]{1,0:T(8,128)(2,1)} fusion(bf16[1408,2048]{1,0:T(8,128)(2,1)} %all-gather.17.cloned.1.call-done, bf16[2048,1408]{1,0:T(8,128)(2,1)} %all-gather.15.cloned.1.call-done, f32[512,1408]{1,0:T(8,128)} %fusion.21, bf16[512,2048]{1,0:T(8,128)(2,1)S(1)} %copy-done.1, f32[2048]{0:T(1024)S(1)} %copy-done.4, ...), kind=kOutput, calls=%fused_computation.27 | convolution fusion | flops 5915148288 | bytes 18622464 | tf_op jit(solution)/shard_map/dot_general | solution.py:23
  490.7 29.5 %reduce-scatter.2.cloned.1.call-done = bf16[512,512]{1,0:T(8,128)(2,1)} async-done(((bf16[512,2048]{1,0:T(8,128)(2,1)}), bf16[512,512]{1,0:T(8,128)(2,1)}) %reduce-scatter.2.cloned.1.call-update) | async-done | bytes 524304 | tf_op jit(solution)/shard_map/reduce_scatter | solution.py:95
  520.2 2.0 add_convert_fusion
  (37 shorter events, 5.2 us)
Async XLA Ops:
  6.5 74.4 %copy-start.3 = (f32[2048]{0:T(1024)S(1)}, f32[2048]{0:T(1024)}, u32[]{:S(2)}) copy-start(f32[2048]{0:T(1024)} %param.11) | copy-start | bytes 24580
  6.5 72.1 %all-gather.7.cloned.1.call-start = ((), (), s32[]{:S(2)}) async-start(), calls=%async_computation.1 | async-start | bytes 2621440 | tf_op jit(solution)/shard_map/all_gather | solution.py:57
  7.3 87.8 %all-gather.9.cloned.1.call-start = ((), (), s32[]{:S(2)}) async-start(), calls=%async_computation.2 | async-start | bytes 2359296 | tf_op jit(solution)/shard_map/all_gather | solution.py:59
  8.0 134.7 %all-gather.11.cloned.1.call-start = ((), (), s32[]{:S(2)}) async-start(), calls=%async_computation.3 | async-start | bytes 2359296 | tf_op jit(solution)/shard_map/all_gather | solution.py:79
  8.7 188.1 %all-reduce.2.cloned.1.call-start = ((), (), s32[]{:S(2)}) async-start(), calls=%async_computation.4 | async-start | bytes 4194304 | tf_op jit(solution)/shard_map/psum | solution.py:82
  78.6 10.2 %copy-start = (bf16[512,2048]{1,0:T(8,128)(2,1)S(1)}, bf16[512,2048]{1,0:T(8,128)(2,1)}, u32[]{:S(2)}) copy-start(bf16[512,2048]{1,0:T(8,128)(2,1)} %all-gather.7.cloned.1.call-done) | copy-start | bytes 6291460
  78.7 10.2 %copy-start.2 = (bf16[2048,128]{1,0:T(8,128)(2,1)S(1)}, bf16[2048,128]{1,0:T(8,128)(2,1)}, u32[]{:S(2)}) copy-start(bf16[2048,128]{1,0:T(8,128)(2,1)} %all_gather.25) | copy-start | bytes 1572868
  83.3 14.8 %collective-permute-start.2 = (bf16[512,128]{1,0:T(8,128)(2,1)S(1)}, bf16[512,128]{1,0:T(8,128)(2,1)S(1)}, u32[]{:S(2)}, u32[]{:S(2)}) collective-permute-start(bf16[512,128]{1,0:T(8,128)(2,1)S(1)} %convolution_convert_fusion.3), channel_id=1, source_target_pairs={{0,8},{4,12},{8,16},{12,20},{16,24},{20,28},{1,9},{5,13},{9,17},{1... | collective-permute-start | bytes 393224 | tf_op jit(solution)/shard_map/ppermute | solution.py:13
  84.6 13.5 %collective-permute-start.3 = (bf16[512,128]{1,0:T(8,128)(2,1)S(1)}, bf16[512,128]{1,0:T(8,128)(2,1)}, u32[]{:S(2)}, u32[]{:S(2)}) collective-permute-start(bf16[512,128]{1,0:T(8,128)(2,1)S(1)} %convolution_convert_fusion.3), channel_id=1, source_target_pairs={{0,4},{4,8},{8,12},{12,16},{16,20},{20,24},{24,28},{1,5},{5,9},{9,... | collective-permute-start | bytes 393224 | tf_op jit(solution)/shard_map/ppermute | solution.py:13
  89.6 14.5 %collective-permute-start = (bf16[512,128]{1,0:T(8,128)(2,1)S(1)}, bf16[512,128]{1,0:T(8,128)(2,1)S(1)}, u32[]{:S(2)}, u32[]{:S(2)}) collective-permute-start(bf16[512,128]{1,0:T(8,128)(2,1)S(1)} %convolution_convert_fusion.4), channel_id=1, source_target_pairs={{0,8},{4,12},{8,16},{12,20},{16,24},{20,28},{1,9},{5,13},{9,17},{1... | collective-permute-start | bytes 393224 | tf_op jit(solution)/shard_map/ppermute | solution.py:13
  92.4 11.8 %collective-permute-start.1 = (bf16[512,128]{1,0:T(8,128)(2,1)S(1)}, bf16[512,128]{1,0:T(8,128)(2,1)S(1)}, u32[]{:S(2)}, u32[]{:S(2)}) collective-permute-start(bf16[512,128]{1,0:T(8,128)(2,1)S(1)} %convolution_convert_fusion.4), channel_id=1, source_target_pairs={{0,4},{4,8},{8,12},{12,16},{16,20},{20,24},{24,28},{1,5},{5,9},{9,... | collective-permute-start | bytes 393224 | tf_op jit(solution)/shard_map/ppermute | solution.py:13
  147.1 144.2 %copy-start.4 = (f32[2048]{0:T(1024)S(1)}, f32[2048]{0:T(1024)}, u32[]{:S(2)}) copy-start(f32[2048]{0:T(1024)} %param.16) | copy-start | bytes 24580
  147.1 144.1 %all-gather.13.cloned.1.call-start = ((), (), s32[]{:S(2)}) async-start(), calls=%async_computation.5 | async-start | bytes 6488064 | tf_op jit(solution)/shard_map/all_gather | solution.py:88
  147.7 236.1 %all-gather.15.cloned.1.call-start = ((), (), s32[]{:S(2)}) async-start(), calls=%async_computation.6 | async-start | bytes 6488064 | tf_op jit(solution)/shard_map/all_gather | solution.py:89
  148.3 328.9 %all-gather.17.cloned.1.call-start = ((), (), s32[]{:S(2)}) async-start(), calls=%async_computation.7 | async-start | bytes 6488064 | tf_op jit(solution)/shard_map/all_gather | solution.py:93
  149.1 371.1 %reduce-scatter.2.cloned.1.call-start = ((), (), s32[]{:S(2)}) async-start(), calls=%async_computation.8 | async-start | bytes 2621440 | tf_op jit(solution)/shard_map/reduce_scatter | solution.py:95
  291.3 185.9 %copy-start.1 = (bf16[512,2048]{1,0:T(8,128)(2,1)S(1)}, bf16[512,2048]{1,0:T(8,128)(2,1)}, u32[]{:S(2)}) copy-start(bf16[512,2048]{1,0:T(8,128)(2,1)} %get-tuple-element.6) | copy-start | bytes 6291460
Sparse Core Ops, SparseCore 0:
  8.9 25.2 all-gather.6
  36.3 52.5 all-gather.8
  91.0 51.7 all-gather.10
  147.3 49.5 all-reduce.1
  198.9 92.3 all-gather.12
  293.3 90.4 all-gather.14
  385.9 91.2 all-gather.16
  490.8 29.3 reduce-scatter.1
where the time goes:
time: 529 us
  waiting for transfers between devices  383 us (72%)
  blocking collectives  68.5 us (13%)
  matrix products  40.5 us (8%)
  between operations  13.7 us (3%)
  other arithmetic  12.2 us (2%)
  starting transfers between devices  11.5 us (2%)
    all_gather x1, waiting for transfers between devices, per_device(): down_full = lax.all_gather(w_down, 'seq', axis=1, tiled=True)  93.4 us
    all_gather x1, waiting for transfers between devices, per_device(): gate_full = lax.all_gather(w_gate, 'seq', axis=0, tiled=True)  90.5 us
    all_gather x1, waiting for transfers between devices, per_device(): up_full = lax.all_gather(w_up, 'seq', axis=0, tiled=True)  84.1 us
    psum x1, waiting for transfers between devices, per_device(): lax.psum(head_terms.astype(jnp.bfloat16), 'tensor').astype(jnp.float32)  47.5 us
    all_gather x1, blocking collectives, per_device(): lax.all_gather(w_value, 'seq', axis=0, tiled=True)  35.2 us
    all_gather x1, waiting for transfers between devices, per_device(): out_full = lax.all_gather(w_out, 'seq', axis=1, tiled=True)  33.7 us
    all_gather x1, blocking collectives, per_device(): lax.all_gather(w_key, 'seq', axis=0, tiled=True)  33.4 us
    dot_general x6, matrix products, product(): return jnp.dot(left, right, preferred_element_type=jnp.float32)  32.3 us
  transfers between devices with their start and end apart: 12, of which 6 were waited for; matrix products, arithmetic and copies ran while one was open for 6% of the time, Pallas kernels for 0%

commit v1 on v0

v1 whole, which is shorter than its diff:
```python
import functools

import jax
import jax.numpy as jnp
from jax import lax
from jax.experimental import pallas as pl
from jax.experimental.pallas import tpu as pltpu
from jax.sharding import Mesh, PartitionSpec as P

HEAD_DIM = 128
WINDOW = 1024


def product(left, right):
    return jnp.dot(left, right, preferred_element_type=jnp.float32)


def traded(block, cut):
    member = lax.axis_index("pair")
    half = block.shape[cut] // 2
    kept = lax.dynamic_slice_in_dim(block, member * half, half, cut)
    given = lax.dynamic_slice_in_dim(block, (1 - member) * half, half, cut)
    got = lax.ppermute(given, "pair", [(0, 1), (1, 0)])
    first = member == 0
    return jnp.concatenate(
        [jnp.where(first, kept, got), jnp.where(first, got, kept)], axis=1 - cut
    )


def attend(queries, keys, values, first_key):
    rows = queries.shape[0]
    span = keys.shape[0]
    group = queries.shape[1] // HEAD_DIM
    block = queries.reshape(rows, group, HEAD_DIM)
    scores = jnp.einsum("qgd,cd->gqc", block, keys, preferred_element_type=jnp.float32)
    scores = scores * HEAD_DIM ** (-0.5)
    query_pos = lax.broadcasted_iota(jnp.int32, (rows, span), 0)
    key_pos = lax.broadcasted_iota(jnp.int32, (rows, span), 1)
    distance = query_pos + WINDOW - key_pos
    allowed = (distance >= 0) & (distance < WINDOW) & (key_pos + first_key >= 0)
    scores = jnp.where(allowed[None], scores, -1e30)
    highest = jnp.max(scores, axis=2, keepdims=True)
    raised = jnp.exp(scores - highest)
    weights = (raised / jnp.sum(raised, axis=2, keepdims=True)).astype(jnp.bfloat16)
    mixed = jnp.einsum("gqc,cd->qgd", weights, values, preferred_element_type=jnp.float32)
    return mixed.astype(jnp.bfloat16).reshape(rows, group * HEAD_DIM)


def places(chips):
    member, at = lax.axis_index("pair"), lax.axis_index("tensor")
    sibling = at + 1 - 2 * lax.rem(at, 2)

    def ahead(k, start):
        return lax.rem(member + k // chips, 2), lax.rem(start + 2 * (k % chips), 2 * chips)

    def behind(k, start):
        turn = 2 * chips - 2 * (k % chips)
        return lax.rem(member + k // chips, 2), lax.rem(start + turn, 2 * chips)

    return member, at, sibling, ahead, behind


def greet(chips, at, sibling, ahead, member):
    barrier = pltpu.get_barrier_semaphore()
    for k in range(1, 2 * chips):
        there = ahead(k, at)
        pl.semaphore_signal(barrier, inc=1, device_id={"pair": there[0], "tensor": there[1]})
    pl.semaphore_signal(barrier, inc=1, device_id={"pair": member, "tensor": sibling})
    pl.semaphore_wait(barrier, 2 * chips)


def sent(source, target, send, recv, where):
    return pltpu.make_async_remote_copy(
        src_ref=source,
        dst_ref=target,
        send_sem=send,
        recv_sem=recv,
        device_id={"pair": where[0], "tensor": where[1]},
    )


def gather_kernel(chips, x_ref, gain_ref, out_ref, held, own, send, recv, pass_send, pass_recv):
    rows, cols = x_ref.shape
    member, at, sibling, ahead, behind = places(chips)

    def block(where):
        return held.at[
            pl.ds(pl.multiple_of(where[0] * rows, rows), rows),
            pl.ds(pl.multiple_of(where[1] * cols, cols), cols),
        ]

    greet(chips, at, sibling, ahead, member)
    count = 2 * chips
    mine = block((member, at))
    copies = [
        sent(x_ref, mine, send.at[k], recv.at[k], ahead(k, at)) for k in range(1, count)
    ]
    for copy in reversed(copies):
        copy.start()
    passed = [sent(x_ref, mine, pass_send.at[0], pass_recv.at[0], (member, sibling))]
    passed[0].start()
    local = pltpu.make_async_copy(x_ref, mine, own)
    local.start()
    for k in range(1, count):
        came = block(behind(k, at))
        sent(came, came, send.at[k], recv.at[k], (member, sibling)).wait_recv()
        onward = sent(came, came, pass_send.at[k], pass_recv.at[k], (member, sibling))
        onward.start()
        passed.append(onward)
    local.wait()
    for k in range(count):
        came = block(behind(k, sibling))
        sent(came, came, pass_send.at[k], pass_recv.at[k], (member, sibling)).wait_recv()
    for copy in copies + passed:
        copy.wait_send()

    step = 32

    @pl.loop(0, 2 * rows // step)
    def _(index):
        at_rows = pl.ds(pl.multiple_of(index * step, step), step)
        values = held[at_rows, :].astype(jnp.float32)
        mean_square = jnp.mean(values * values, axis=1, keepdims=True)
        scaled = values * lax.rsqrt(mean_square + 1e-06) * gain_ref[...]
        out_ref[at_rows, :] = scaled.astype(out_ref.dtype)


def normed_rows(share, gain, chips, identity):
    rows, cols = share.shape
    count = 2 * chips
    size = (2 * rows, count * cols)
    vmem = pl.BlockSpec(memory_space=pltpu.VMEM)
    return pl.pallas_call(
        functools.partial(gather_kernel, chips),
        out_shape=jax.ShapeDtypeStruct(size, jnp.bfloat16),
        in_specs=[vmem] * 2,
        out_specs=vmem,
        scratch_shapes=[
            pltpu.VMEM(size, jnp.bfloat16),
            pltpu.SemaphoreType.DMA,
            pltpu.SemaphoreType.DMA((count,)),
            pltpu.SemaphoreType.DMA((count,)),
            pltpu.SemaphoreType.DMA((count,)),
            pltpu.SemaphoreType.DMA((count,)),
        ],
        cost_estimate=pl.CostEstimate(
            flops=60 * size[0] * size[1], bytes_accessed=20 * size[0] * size[1], transcendentals=0
        ),
        compiler_params=pltpu.CompilerParams(collective_id=identity, has_side_effects=True),
    )(share, gain.reshape(1, -1))


def sum_kernel(
    chips, terms, base, out_ref, near, stage, far, near_send, near_recv, send, recv
):
    rows, cols = base.shape
    member, at, sibling, ahead, behind = places(chips)
    count = 2 * chips

    def block(where):
        return terms.at[
            pl.ds(pl.multiple_of(where[0] * rows, rows), rows),
            pl.ds(pl.multiple_of(where[1] * cols, cols), cols),
        ]

    greet(chips, at, sibling, ahead, member)
    order = list(range(count - 1, -1, -1))
    given = {
        k: sent(
            block(ahead(k, sibling)),
            near.at[k],
            near_send.at[k],
            near_recv.at[k],
            (member, sibling),
        )
        for k in order
    }
    for k in order:
        given[k].start()
    step = 64
    copies = {}
    for k in order:
        given[k].wait_recv()
        own = block(ahead(k, at))

        @pl.loop(0, rows // step)
        def _(index, k=k, own=own):
            part = pl.ds(pl.multiple_of(index * step, step), step)
            total = own[part, :].astype(jnp.float32) + near[k, part, :].astype(jnp.float32)
            stage[k, part, :] = total.astype(jnp.bfloat16)

        if k:
            copies[k] = sent(stage.at[k], far.at[k], send.at[k], recv.at[k], ahead(k, at))
            copies[k].start()
    for k in order[:-1]:
        copies[k].wait_recv()

    @pl.loop(0, rows // step)
    def _(index):
        part = pl.ds(pl.multiple_of(index * step, step), step)
        total = stage[0, part, :].astype(jnp.float32)
        for k in range(1, count):
            total = total + far[k, part, :].astype(jnp.float32)
        out_ref[part, :] = (base[part, :].astype(jnp.float32) + total).astype(out_ref.dtype)

    for k in order:
        given[k].wait_send()
        if k:
            copies[k].wait_send()


def added_share(terms, base, chips, identity):
    rows, cols = base.shape
    count = 2 * chips
    vmem = pl.BlockSpec(memory_space=pltpu.VMEM)
    slots = pltpu.VMEM((count, rows, cols), jnp.bfloat16)
    return pl.pallas_call(
        functools.partial(sum_kernel, chips),
        out_shape=jax.ShapeDtypeStruct(base.shape, jnp.bfloat16),
        in_specs=[vmem] * 2,
        out_specs=vmem,
        scratch_shapes=[slots] * 3 + [pltpu.SemaphoreType.DMA((count,))] * 4,
        cost_estimate=pl.CostEstimate(
            flops=60 * terms.size, bytes_accessed=20 * terms.size, transcendentals=0
        ),
        compiler_params=pltpu.CompilerParams(collective_id=identity, has_side_effects=True),
    )(terms, base)


def per_device(tokens, attn_gain, w_query, w_key, w_value, w_out, mlp_gain, w_gate, w_up, w_down):
    rows = tokens.shape[0]
    hi, member = lax.axis_index("hi"), lax.axis_index("pair")
    runs = lax.axis_size("hi")
    swap = [(0, 1), (1, 0)]
    first = member == 0
    kept = jnp.where(first, w_key, w_value)
    got = lax.ppermute(jnp.where(first, w_value, w_key), "pair", swap)
    pair_rows = [jnp.where(first, kept, got), jnp.where(first, got, kept)]
    kv_rows = jnp.concatenate(pair_rows, axis=0)
    qkv = jnp.concatenate([traded(w_query, 1), kv_rows], axis=1)
    qkv_full = lax.all_gather(qkv, "hi", axis=0, tiled=True)
    out_full = lax.all_gather(traded(w_out, 0), "hi", axis=1, tiled=True)
    gate_up = jnp.concatenate([traded(w_gate, 1), traded(w_up, 1)], axis=1)
    gate_up_full = lax.all_gather(gate_up, "hi", axis=0, tiled=True)
    down_full = lax.all_gather(traded(w_down, 0), "hi", axis=1, tiled=True)

    chips = lax.axis_size("tensor") // 2
    normed = normed_rows(tokens, attn_gain, chips, 1)
    width = w_query.shape[1] // 2
    projected = product(normed, qkv_full).astype(jnp.bfloat16)
    queries, mine = projected[:, :width], projected[:, width:]
    other = lax.ppermute(mine, "pair", swap)
    onward = [(i, i + 1) for i in range(runs - 1)]
    across = [
        (i * 2 + m, (i + 1) * 2 + 1 - m) for i in range(runs - 1) for m in range(2)
    ]
    mine_before = lax.ppermute(mine, "hi", onward)
    other_before = lax.ppermute(mine, ("hi", "pair"), across)
    mine = jnp.concatenate([mine_before, mine], axis=0)
    other = jnp.concatenate([other_before, other], axis=0)
    keys = jnp.where(first, mine, other)
    values = jnp.where(first, other, mine)
    blocks = []
    before = 2 * rows
    for at in range(0, 2 * rows, rows):
        start = before + at - WINDOW
        stop = before + at + rows
        blocks.append(
            attend(
                queries[at : at + rows],
                keys[start:stop],
                values[start:stop],
                (hi - 1) * before + start,
            )
        )
    attended = jnp.concatenate(blocks, axis=0)
    attn_terms = product(attended, out_full).astype(jnp.bfloat16)
    stream = added_share(attn_terms, tokens, chips, 2)
    stream_normed = normed_rows(stream, mlp_gain, chips, 3)
    units = gate_up_full.shape[1] // 2
    gate_upward = product(stream_normed, gate_up_full)
    gate, upward = gate_upward[:, :units], gate_upward[:, units:]
    hidden = (jax.nn.silu(gate) * upward).astype(jnp.bfloat16)
    return added_share(product(hidden, down_full).astype(jnp.bfloat16), stream, chips, 4)


def solution(mesh):
    sizes = mesh.shape
    split = Mesh(
        mesh.devices.reshape(sizes["seq"] // 2, 2, sizes["tensor"]), ("hi", "pair", "tensor")
    )
    seq = ("hi", "pair")
    in_specs = (
        P(seq, "tensor"),
        P(),
        P(seq, "tensor"),
        P(seq, "tensor"),
        P(seq, "tensor"),
        P("tensor", seq),
        P(),
        P(seq, "tensor"),
        P(seq, "tensor"),
        P("tensor", seq),
    )
    return jax.shard_map(
        per_device, mesh=split, in_specs=in_specs, out_specs=P(seq, "tensor"), check_vma=False
    )
```

time: 529 us -> 312 us (0.59)
  waiting for transfers between devices: 383 us -> 80.6 us
  Pallas kernels: 0 us -> 138 us
  blocking collectives: 68.5 us -> 0 us
  local copies, waits for them, and re-layouts: 0.02 us -> 7.57 us
  starting transfers between devices: 11.5 us -> 18.1 us
    all_gather x6 -> x4, waiting for transfers between devices: 302 us -> 47.5 us  [the longest x1 47.5 us: per_device(): down_full = lax.all_gather(traded(w_down, 0), 'hi', axis=1, tiled=True)]
    pallas_call x0 -> x4, Pallas kernels: none -> 138 us  [the longest x2 75.1 us: normed_rows(): pl.pallas_call(functools.partial(gather_kernel, chips), out_shape=jax.Sha...]
    all_gather x2 -> x0, blocking collectives: 68.5 us -> none  [the longest x1 35.2 us: per_device(): lax.all_gather(w_value, 'seq', axis=0, tiled=True)]
    psum x1 -> x0, waiting for transfers between devices: 47.5 us -> none  [per_device(): lax.psum(head_terms.astype(jnp.bfloat16), 'tensor').astype(jnp.float32)]
    ppermute x4 -> x9, waiting for transfers between devices: 0.01 us -> 33 us  [the longest x5 16.7 us: traded(): got = lax.ppermute(given, 'pair', [(0, 1), (1, 0)])]
    reduce_scatter x1 -> x0, waiting for transfers between devices: 29.5 us -> none  [per_device(): lax.psum_scatter(unit_terms.astype(jnp.bfloat16), 'tensor', scatter_dimen...]
    reduce_sum x3 -> x0, other arithmetic: 8.89 us -> none  [the longest x2 6.13 us: scaled_rows(): mean_square = jnp.mean(values * values, axis=1, keepdims=True)]
    ppermute x4 -> x9, starting transfers between devices: 11 us -> 18 us  [the longest x5 8.93 us: traded(): got = lax.ppermute(given, 'pair', [(0, 1), (1, 0)])]
  transfers between devices with their start and end apart: 12 -> 13, of which waited for: 6 -> 7; matrix products, arithmetic and copies ran while one was open for 6% -> 15% of each run, Pallas kernels for 0% -> 34%
where the time goes in v1:
time: 312 us; the launch traced here: 311 us
  Pallas kernels  138 us (44%)
  waiting for transfers between devices  80.6 us (26%)
  matrix products  43.5 us (14%)
  starting transfers between devices  18.1 us (6%)
  between operations  13.4 us (4%)
  other arithmetic  10.2 us (3%)
  local copies, waits for them, and re-layouts  7.57 us (2%)
    pallas_call x2, Pallas kernels, normed_rows(): pl.pallas_call(functools.partial(gather_kernel, chips), out_shape=jax.Sha...  75.1 us
    pallas_call x2, Pallas kernels, added_share(): pl.pallas_call(functools.partial(sum_kernel, chips), out_shape=jax.ShapeD...  62.6 us
    all_gather x1, waiting for transfers between devices, per_device(): down_full = lax.all_gather(traded(w_down, 0), 'hi', axis=1, tiled=True)  47.5 us
    dot_general x4, matrix products, product(): return jnp.dot(left, right, preferred_element_type=jnp.float32)  30.2 us
    ppermute x5, waiting for transfers between devices, traded(): got = lax.ppermute(given, 'pair', [(0, 1), (1, 0)])  16.7 us
    ppermute x1, waiting for transfers between devices, per_device(): mine_before = lax.ppermute(mine, 'hi', onward)  9.64 us
    ppermute x5, starting transfers between devices, traded(): got = lax.ppermute(given, 'pair', [(0, 1), (1, 0)])  8.93 us
    dot_general x2, matrix products, attend(): jnp.einsum('gqc,cd->qgd', weights, values, preferred_element_type=jnp.flo...  7.33 us
  transfers between devices with their start and end apart: 13, of which 7 were waited for; matrix products, arithmetic and copies ran while one was open for 15% of the time, Pallas kernels for 34%

profile of v1, /device:TPU:0, one launch (start us, length us, event | category | flops | bytes accessed | tf_op | source)
XLA Modules:
  0.0 311.1 jit_solution(1343620643643725484)
XLA Ops:
  7.6 3.0 collective-permute-start
  12.5 2.1 collective-permute-start.5
  14.5 2.0 collective-permute-done.1
  25.0 9.2 %collective-permute-done.6 = bf16[256,704]{1,0:T(8,128)(2,1)S(1)} collective-permute-done((bf16[256,704]{1,0:T(8,128)(2,1)}, bf16[256,704]{1,0:T(8,128)(2,1)S(1)}, u32[]{:S(2)}, u32[]{:S(2)}) %collective-permute-start.6) | collective-permute-done | bytes 360480 | tf_op jit(solution)/shard_map/ppermute | solution.py:23
  34.5 6.5 %collective-permute-done.7 = bf16[256,704]{1,0:T(8,128)(2,1)S(1)} collective-permute-done((bf16[256,704]{1,0:T(8,128)(2,1)}, bf16[256,704]{1,0:T(8,128)(2,1)S(1)}, u32[]{:S(2)}, u32[]{:S(2)}) %collective-permute-start.7) | collective-permute-done | bytes 360480 | tf_op jit(solution)/shard_map/ppermute | solution.py:23
  42.9 1.8 collective-permute-start.8
  44.7 38.3 %shard_map.100 = bf16[1024,2048]{1,0:T(8,128)(2,1)} custom-call(bf16[512,512]{1,0:T(8,128)(2,1)} %base.1, f32[1,2048]{1,0:T(1,128)} %bitcast.80), custom_call_target="tpu_custom_call" | custom-call | flops 125829120 | bytes 41943040 | tf_op jit(solution)/shard_map/pallas_call | solution.py:133
  85.8 4.5 %convolution_convert_fusion.2 = bf16[1024,384]{0,1:T(8,128)(2,1)S(1)} fusion(bf16[1024,2048]{1,0:T(8,128)(2,1)} %shard_map.100, bf16[2048,384]{1,0:T(8,128)(2,1)} %all-gather.5.cloned.1.call-done), kind=kOutput, calls=%fused_computation.30 | convolution fusion | flops 1611005952 | bytes 6553600 | tf_op jit(solution)/shard_map/dot_general | solution.py:15
  90.3 5.4 %collective-permute-start.2 = (bf16[1024,128]{0,1:T(8,128)(2,1)S(1)}, bf16[1024,128]{0,1:T(8,128)(2,1)}, u32[]{:S(2)}, u32[]{:S(2)}) collective-permute-start(bf16[1024,128]{0,1:T(8,128)(2,1)S(1)} %slice.39), channel_id=1, source_target_pairs={{0,12},{4,8},{8,20},{12,16},{16,28},{20,24},{1,13},{5,9},{9,21},{1... | collective-permute-start | bytes 786440 | tf_op jit(solution)/shard_map/ppermute | solution.py:258
  97.2 3.0 collective-permute-start.4
  101.0 4.7 %collective-permute-done.2 = bf16[1024,128]{0,1:T(8,128)(2,1)} collective-permute-done((bf16[1024,128]{0,1:T(8,128)(2,1)S(1)}, bf16[1024,128]{0,1:T(8,128)(2,1)}, u32[]{:S(2)}, u32[]{:S(2)}) %collective-permute-start.2) | collective-permute-done | bytes 262176 | tf_op jit(solution)/shard_map/ppermute | solution.py:258
  106.8 9.6 %collective-permute-done.4 = bf16[1024,128]{0,1:T(8,128)(2,1)S(1)} collective-permute-done((bf16[1024,128]{0,1:T(8,128)(2,1)S(1)}, bf16[1024,128]{0,1:T(8,128)(2,1)S(1)}, u32[]{:S(2)}, u32[]{:S(2)}) %collective-permute-start.4) | collective-permute-done | bytes 262176 | tf_op jit(solution)/shard_map/ppermute | solution.py:257
  116.7 3.5 %fusion.49 = f32[2,512]{1,0:T(2,128)S(1)} fusion(pred[512,1536]{0,1:T(8,128)(4,1)S(1)} %get-tuple-element.21, bf16[512,2,128]{0,2,1:T(8,128)(2,1)} %bitcast.78, bf16[2048,128]{0,1:T(8,128)(2,1)S(1)} %get-tuple-element.12), kind=kOutput, calls=%fused_computation.88 | convolution fusion | flops 408946176 | bytes 1445888 | tf_op jit(solution)/shard_map/sub | solution.py:43
  120.2 4.2 %fusion.21 = bf16[128,2,512]{2,0,1:T(8,128)(2,1)S(1)} fusion(f32[2,512]{1,0:T(2,128)S(1)} %fusion.49, bf16[2048,128]{0,1:T(8,128)(2,1)S(1)} %get-tuple-element.11, pred[512,1536]{0,1:T(8,128)(4,1)S(1)} %get-tuple-element.21, bf16[512,2,128]{0,2,1:T(8,128)(2,1)} %bitcast.79, bf16[2048,128]{0,1:T(8,128)(2,1)S(1)} %get-tuple-element.12), kind=kOutput, calls=%fused_computation.32 | convolution fusion | flops 813304320 | bytes 2101248 | tf_op jit(solution)/shard_map/gqc,cd->qgd/dot_general | solution.py:45
  124.3 2.5 fusion.48
  126.9 3.2 %fusion.20 = bf16[128,2,512]{2,0,1:T(8,128)(2,1)S(1)} fusion(f32[2,512]{1,0:T(2,128)S(1)} %fusion.48, bf16[2048,128]{0,1:T(8,128)(2,1)S(1)} %get-tuple-element.11, pred[512,1536]{0,1:T(8,128)(4,1)S(1)} %get-tuple-element.22, bf16[512,2,128]{0,2,1:T(8,128)(2,1)S(1)} %bitcast.77, bf16[2048,128]{0,1:T(8,128)(2,1)S(1)} %get-tuple-element.12), kind=kOutput, calls=%fused_computation.31 | convolution fusion | flops 813304320 | bytes 2101248 | tf_op jit(solution)/shard_map/gqc,cd->qgd/dot_general | solution.py:45
  130.1 4.8 %convolution_convert_fusion.1.terms = bf16[1024,2048]{1,0:T(8,128)(2,1)} fusion(bf16[256,2048]{1,0:T(8,128)(2,1)} %all-gather.7.cloned.1.call-done, bf16[512,256]{0,1:T(8,128)(2,1)S(1)} %bitcast.75, bf16[512,256]{0,1:T(8,128)(2,1)S(1)} %bitcast.74), kind=kOutput, calls=%fused_computation.11 | convolution fusion | flops 1076887552 | bytes 5767168 | tf_op jit(solution)/shard_map/dot_general | solution.py:15
  134.8 30.7 %shard_map.101.x_ref.base = bf16[512,512]{1,0:T(8,128)(2,1)} custom-call(bf16[1024,2048]{1,0:T(8,128)(2,1)} %convolution_convert_fusion.1.terms, bf16[512,512]{1,0:T(8,128)(2,1)} %base.1), custom_call_target="tpu_custom_call" | custom-call | flops 125829120 | bytes 41943040 | tf_op jit(solution)/shard_map/pallas_call | solution.py:217
  165.6 36.8 %shard_map.102 = bf16[1024,2048]{1,0:T(8,128)(2,1)} custom-call(bf16[512,512]{1,0:T(8,128)(2,1)} %shard_map.101.x_ref.base, f32[1,2048]{1,0:T(1,128)} %bitcast.81), custom_call_target="tpu_custom_call" | custom-call | flops 125829120 | bytes 41943040 | tf_op jit(solution)/shard_map/pallas_call | solution.py:133
  202.5 11.7 %fusion.50 = f32[1024,1408]{1,0:T(8,128)} fusion(bf16[1024,2048]{1,0:T(8,128)(2,1)} %shard_map.102, bf16[2048,1408]{1,0:T(8,128)(2,1)} %all-gather.9.cloned.1.call-done), kind=kOutput, calls=%fused_computation.89 | convolution fusion | flops 5905580032 | bytes 15728640 | tf_op jit(solution)/shard_map/dot_general | solution.py:15
  214.2 47.5 %all-gather.11.cloned.1.call-done = bf16[704,2048]{1,0:T(8,128)(2,1)} async-done(((bf16[704,512]{1,0:T(8,128)(2,1)}), bf16[704,2048]{1,0:T(8,128)(2,1)}) %all-gather.11.cloned.1.call-update) | async-done | bytes 2883600 | tf_op jit(solution)/shard_map/all_gather | solution.py:245
  261.7 9.1 %convolution_convert_fusion.terms = bf16[1024,2048]{1,0:T(8,128)(2,1)} fusion(bf16[704,2048]{1,0:T(8,128)(2,1)} %all-gather.11.cloned.1.call-done, f32[1024,1408]{1,0:T(8,128)} %fusion.50), kind=kOutput, calls=%fused_computation.10 | convolution fusion | flops 2959212544 | bytes 13369344 | tf_op jit(solution)/shard_map/dot_general | solution.py:15
  270.8 31.9 %shard_map.103 = bf16[512,512]{1,0:T(8,128)(2,1)} custom-call(bf16[1024,2048]{1,0:T(8,128)(2,1)} %convolution_convert_fusion.terms, bf16[512,512]{1,0:T(8,128)(2,1)} %shard_map.101.x_ref.base), custom_call_target="tpu_custom_call" | custom-call | flops 125829120 | bytes 41943040 | tf_op jit(solution)/shard_map/pallas_call | solution.py:217
  302.7 1.9 copy.27
  (51 shorter events, 19.9 us)
Async XLA Ops:
  6.5 14.5 %copy-start = (bf16[256,1408]{1,0:T(8,128)(2,1)S(1)}, bf16[256,1408]{1,0:T(8,128)(2,1)}, u32[]{:S(2)}) copy-start(bf16[256,1408]{1,0:T(8,128)(2,1)} %param.17) | copy-start | bytes 2162692
  6.5 17.2 %copy-start.1 = (bf16[256,1408]{1,0:T(8,128)(2,1)S(1)}, bf16[256,1408]{1,0:T(8,128)(2,1)}, u32[]{:S(2)}) copy-start(bf16[256,1408]{1,0:T(8,128)(2,1)} %param.18) | copy-start | bytes 2162692
  6.5 79.2 %all-gather.5.cloned.1.call-start = ((), (), s32[]{:S(2)}) async-start(), calls=%async_computation | async-start | bytes 1966080 | tf_op jit(solution)/shard_map/all_gather | solution.py:241
  7.6 9.8 %collective-permute-start = (bf16[256,256]{1,0:T(8,128)(2,1)S(1)}, bf16[256,256]{1,0:T(8,128)(2,1)S(1)}, u32[]{:S(2)}, u32[]{:S(2)}) collective-permute-start(bf16[256,256]{1,0:T(8,128)(2,1)S(1)} %constant_dynamic-slice_fusion.4), channel_id=1, source_target_pairs={{0,4},{4,0},{1,5},{5,1},{2,6},{6,2},{3,7},{7,3},{8,12},{12,8},{9,1... | collective-permute-start | bytes 393224 | tf_op jit(solution)/shard_map/ppermute | solution.py:23
  11.5 5.0 %collective-permute-start.1 = (bf16[256,128]{1,0:T(8,128)(2,1)S(1)}, bf16[256,128]{1,0:T(8,128)(2,1)S(1)}, u32[]{:S(2)}, u32[]{:S(2)}) collective-permute-start(bf16[256,128]{1,0:T(8,128)(2,1)S(1)} %broadcast_select_fusion.14), channel_id=1, source_target_pairs={{0,4},{4,0},{1,5},{5,1},{2,6},{6,2},{3,7},{7,3},{8,12},{12,8},{9,1... | collective-permute-start | bytes 196616 | tf_op jit(solution)/shard_map/ppermute | solution.py:237
  12.5 5.8 %collective-permute-start.5 = (bf16[256,256]{1,0:T(8,128)(2,1)S(1)}, bf16[256,256]{1,0:T(8,128)(2,1)S(1)}, u32[]{:S(2)}, u32[]{:S(2)}) collective-permute-start(bf16[256,256]{1,0:T(8,128)(2,1)S(1)} %constant_dynamic-slice_fusion.3), channel_id=1, source_target_pairs={{0,4},{4,0},{1,5},{5,1},{2,6},{6,2},{3,7},{7,3},{8,12},{12,8},{9,1... | collective-permute-start | bytes 393224 | tf_op jit(solution)/shard_map/ppermute | solution.py:23
  20.2 109.9 %all-gather.7.cloned.1.call-start = ((), (), s32[]{:S(2)}) async-start(), calls=%async_computation.1 | async-start | bytes 1310720 | tf_op jit(solution)/shard_map/all_gather | solution.py:242
  21.0 181.5 %all-gather.9.cloned.1.call-start = ((), (), s32[]{:S(2)}) async-start(), calls=%async_computation.2 | async-start | bytes 7208960 | tf_op jit(solution)/shard_map/all_gather | solution.py:244
  22.0 20.8 %copy-start.2 = (bf16[1408,256]{1,0:T(8,128)(2,1)S(1)}, bf16[1408,256]{1,0:T(8,128)(2,1)}, u32[]{:S(2)}) copy-start(bf16[1408,256]{1,0:T(8,128)(2,1)} %param.19) | copy-start | bytes 2162692
  22.0 12.2 %collective-permute-start.6 = (bf16[256,704]{1,0:T(8,128)(2,1)}, bf16[256,704]{1,0:T(8,128)(2,1)S(1)}, u32[]{:S(2)}, u32[]{:S(2)}) collective-permute-start(bf16[256,704]{1,0:T(8,128)(2,1)} %constant_dynamic-slice_fusion.2), channel_id=1, source_target_pairs={{0,4},{4,0},{1,5},{5,1},{2,6},{6,2},{3,7},{7,3},{8,12},{12,8},{9,1... | collective-permute-start | bytes 1081352 | tf_op jit(solution)/shard_map/ppermute | solution.py:23
  24.7 16.2 %collective-permute-start.7 = (bf16[256,704]{1,0:T(8,128)(2,1)}, bf16[256,704]{1,0:T(8,128)(2,1)S(1)}, u32[]{:S(2)}, u32[]{:S(2)}) collective-permute-start(bf16[256,704]{1,0:T(8,128)(2,1)} %constant_dynamic-slice_fusion.1), channel_id=1, source_target_pairs={{0,4},{4,0},{1,5},{5,1},{2,6},{6,2},{3,7},{7,3},{8,12},{12,8},{9,1... | collective-permute-start | bytes 1081352 | tf_op jit(solution)/shard_map/ppermute | solution.py:23
  42.8 218.9 %all-gather.11.cloned.1.call-start = ((), (), s32[]{:S(2)}) async-start(), calls=%async_computation.3 | async-start | bytes 3604480 | tf_op jit(solution)/shard_map/all_gather | solution.py:245
  42.9 41.8 %collective-permute-start.8 = (bf16[704,256]{1,0:T(8,128)(2,1)S(1)}, bf16[704,256]{1,0:T(8,128)(2,1)}, u32[]{:S(2)}, u32[]{:S(2)}) collective-permute-start(bf16[704,256]{1,0:T(8,128)(2,1)S(1)} %constant_dynamic-slice_fusion), channel_id=1, source_target_pairs={{0,4},{4,0},{1,5},{5,1},{2,6},{6,2},{3,7},{7,3},{8,12},{12,8},{9,1... | collective-permute-start | bytes 1081352 | tf_op jit(solution)/shard_map/ppermute | solution.py:23
  90.3 15.5 %collective-permute-start.2 = (bf16[1024,128]{0,1:T(8,128)(2,1)S(1)}, bf16[1024,128]{0,1:T(8,128)(2,1)}, u32[]{:S(2)}, u32[]{:S(2)}) collective-permute-start(bf16[1024,128]{0,1:T(8,128)(2,1)S(1)} %slice.39), channel_id=1, source_target_pairs={{0,12},{4,8},{8,20},{12,16},{16,28},{20,24},{1,13},{5,9},{9,21},{1... | collective-permute-start | bytes 786440 | tf_op jit(solution)/shard_map/ppermute | solution.py:258
  96.6 10.1 %collective-permute-start.3 = (bf16[1024,128]{0,1:T(8,128)(2,1)S(1)}, bf16[1024,128]{0,1:T(8,128)(2,1)S(1)}, u32[]{:S(2)}, u32[]{:S(2)}) collective-permute-start(bf16[1024,128]{0,1:T(8,128)(2,1)S(1)} %slice.39), channel_id=1, source_target_pairs={{0,4},{4,0},{1,5},{5,1},{2,6},{6,2},{3,7},{7,3},{8,12},{12,8},{9,1... | collective-permute-start | bytes 786440 | tf_op jit(solution)/shard_map/ppermute | solution.py:252
  97.2 19.2 %collective-permute-start.4 = (bf16[1024,128]{0,1:T(8,128)(2,1)S(1)}, bf16[1024,128]{0,1:T(8,128)(2,1)S(1)}, u32[]{:S(2)}, u32[]{:S(2)}) collective-permute-start(bf16[1024,128]{0,1:T(8,128)(2,1)S(1)} %slice.39), channel_id=1, source_target_pairs={{0,8},{8,16},{16,24},{1,9},{9,17},{17,25},{2,10},{10,18},{18,26},{... | collective-permute-start | bytes 786440 | tf_op jit(solution)/shard_map/ppermute | solution.py:257
  120.2 4.2 %copy-start.3 = (bf16[512,256]{0,1:T(8,128)(2,1)S(1)}, bf16[512,256]{0,1:T(8,128)(2,1)}, u32[]{:S(2)}) copy-start(bf16[512,256]{0,1:T(8,128)(2,1)} %get-tuple-element.14) | copy-start | bytes 786436
Sparse Core Ops, SparseCore 0:
  20.3 38.5 all-gather.4
  60.4 26.8 all-gather.6
  88.9 111.0 all-gather.8
  201.4 60.2 all-gather.10
